TPU v7x, 32 devices: a whole 2x2x4 slice. The times are simulated.
32 devices in a mesh: seq: 8 (over z, core), fsdp: 4 (over y, x).
Axes of the slice: x: 2, y: 2, z: 4, core: 2. Of those that a mesh axis runs over, the one named last changes fastest.
Arguments:
- tokens: bfloat16 [4, 1024, 2048], P('fsdp', 'seq'), may hold values from -6 to 6
- ln_gain: bfloat16 [2048], P('fsdp'), may hold values from 0.5 to 1.5
- ln_bias: bfloat16 [2048], P('fsdp'), may hold values from -3 to 3
- qkv_weight: bfloat16 [2048, 6144], P('fsdp')
- qkv_bias: bfloat16 [6144], P('fsdp'), may hold values from -3 to 3
- dense_weight: bfloat16 [2048, 2048], P('fsdp'), may hold values from -0.5 to 0.5
- dense_bias: bfloat16 [2048], P('fsdp'), may hold values from -3 to 3
- fc1_weight: bfloat16 [2048, 8192], P('fsdp'), may hold values from -0.125 to 0.125
- fc1_bias: bfloat16 [8192], P('fsdp'), may hold values from -3 to 3
- fc2_weight: bfloat16 [8192, 2048], P('fsdp'), may hold values from -0.0625 to 0.0625
- fc2_bias: bfloat16 [2048], P('fsdp'), may hold values from -3 to 3
- segments: int32 [4, 1024], P('fsdp'), may hold values from 0 to 1, as said below
- positions: int32 [4, 1024], P('fsdp', 'seq'), may hold values from 0 to 2046, as said below
- cotangent: bfloat16 [4, 1024, 2048], P('fsdp', 'seq'), may hold values from -6 to 6
Outputs:
- out: bfloat16 [4, 1024, 2048], P('fsdp', 'seq')
- grad_tokens: float32 [4, 1024, 2048], P('fsdp', 'seq')
- grad_ln_gain: float32 [2048], P('fsdp')
- grad_ln_bias: float32 [2048], P('fsdp')
- grad_qkv_weight: float32 [2048, 6144], P('fsdp')
- grad_qkv_bias: float32 [6144], P('fsdp')
- grad_dense_weight: float32 [2048, 2048], P('fsdp')
- grad_dense_bias: float32 [2048], P('fsdp')
- grad_fc1_weight: float32 [2048, 8192], P('fsdp')
- grad_fc1_bias: float32 [8192], P('fsdp')
- grad_fc2_weight: float32 [8192, 2048], P('fsdp')
- grad_fc2_bias: float32 [2048], P('fsdp')
Inputs may be any that keep to these rules, and one draw needn't show every extreme that they name: `segments`: document numbers never fall along a sequence and each of 0 to 1 occurs in every sequence. The first document of each sequence starts at position 0; positions rise by one from token to token within a document; in every sequence the last token of the last document has position 2046.
All inputs are finite; a program needn't handle non-finite values.
Results may differ from a plain program's by a relative error of at most 0.0095.
Values may be sent and summed in bfloat16 or wider, within the bound.
A program may use at most 448 MiB of HBM per device.

v0:
```python
import functools

import jax
import jax.numpy as jnp
from jax import lax
from jax.experimental import pallas as pl
from jax.experimental.pallas import tpu as pltpu
from jax.sharding import PartitionSpec as P


HEADS = 32
HEAD = 64
ROT = 32
EPS = 1e-05
DOC_SHIFT = 1023
LANES = 2 * HEAD
BF = jnp.bfloat16
F32 = jnp.float32


def dot(left, right):
    return lax.dot_general(left, right, (((1,), (0,)), ((), ())), preferred_element_type=F32)


def dot_nt(left, right):
    return lax.dot_general(left, right, (((1,), (1,)), ((), ())), preferred_element_type=F32)


def dot_tn(left, right):
    return lax.dot_general(left, right, (((0,), (0,)), ((), ())), preferred_element_type=F32)


def columns(ref, cols):
    if len(ref.shape) == 2:
        return ref[:, cols]
    block = ref[:, :, cols]
    return block.reshape(-1, block.shape[-1])


def gelu_tanh(values_in):
    return jax.nn.gelu(values_in, approximate=True)


def turn(values, cos, sin_low, sin_high):
    half = ROT // 2
    return (
        values * cos
        - pltpu.roll(values, LANES - half, 1) * sin_low
        + pltpu.roll(values, half, 1) * sin_high
    )


def attention_kernel(
    rows, proj, grad_out, cos, sin_low, sin_high, seg_col, seg_row,
    out, grad_proj, qs, ks, vs, dk, dv, pause=None,
):
    length = proj.shape[0]
    blocks = length // rows
    scale = HEAD**-0.5
    for i in range(blocks):
        r = slice(i * rows, (i + 1) * rows)
        c, lo, hi = cos[r, :], sin_low[r, :], sin_high[r, :]
        qs[r, :] = turn(proj[r, 0:LANES], c, lo, hi).astype(BF) * jnp.asarray(scale, BF)
        ks[r, :] = turn(proj[r, LANES : 2 * LANES], c, lo, hi).astype(BF)
        vs[r, :] = proj[r, 2 * LANES : 3 * LANES].astype(BF)
    lane = lax.broadcasted_iota(jnp.int32, (rows, LANES), 1)
    first = lane < HEAD
    zero = jnp.zeros((rows, LANES), BF)
    for i in reversed(range(blocks)):
        r = slice(i * rows, (i + 1) * rows)
        n = (i + 1) * rows
        place_q = i * rows + lax.broadcasted_iota(jnp.int32, (rows, n), 0)
        place_k = lax.broadcasted_iota(jnp.int32, (rows, n), 1)
        allowed = (place_k <= place_q) & (seg_col[r, :] == seg_row[:, 0:n])
        q2, g2 = qs[r, :], grad_out[r, :]
        k, v = ks[0:n, :], vs[0:n, :]
        o_parts, dq_parts = [], []
        for h in range(2):
            mine = first if h == 0 else ~first
            q = jnp.where(mine, q2, zero)
            g = jnp.where(mine, g2, zero)
            s = jnp.where(allowed, dot_nt(q, k), -1e30)
            e = jnp.exp(s - jnp.max(s, axis=-1, keepdims=True))
            p = e * (1.0 / jnp.sum(e, axis=-1, keepdims=True))
            pb = p.astype(BF)
            o_parts.append(dot(pb, v))
            dp = dot_nt(g, v)
            inner = jnp.sum(p * dp, axis=-1, keepdims=True)
            ds = (p * (dp - inner)).astype(BF)
            dq_parts.append(dot(ds, k))
            dk_new, dv_new = dot_tn(ds, q), dot_tn(pb, g)
            if i == blocks - 1 and h == 0:
                dk[...] = dk_new
                dv[...] = dv_new
            else:
                dk[0:n, :] += dk_new
                dv[0:n, :] += dv_new
        out[r, :] = jnp.where(first, o_parts[0], o_parts[1]).astype(BF)
        dq = (jnp.where(first, dq_parts[0], dq_parts[1]) * scale).astype(BF).astype(F32)
        c, lo, hi = cos[r, :], sin_low[r, :], sin_high[r, :]
        grad_proj[r, 0:LANES] = turn(dq, c, -lo, -hi).astype(BF)
        if pause is not None:
            pause(i)
    for i in range(blocks):
        r = slice(i * rows, (i + 1) * rows)
        c, lo, hi = cos[r, :], sin_low[r, :], sin_high[r, :]
        grad_k = dk[r, :].astype(BF).astype(F32)
        grad_proj[r, LANES : 2 * LANES] = turn(grad_k, c, -lo, -hi).astype(BF)
        grad_proj[r, 2 * LANES : 3 * LANES] = dv[r, :].astype(BF)


def attention(proj, grad_att, tables, segments):
    length = proj.shape[0]
    pairs = grad_att.shape[1] // LANES
    rows = 256
    whole = lambda shape: pl.BlockSpec(shape, lambda p: (0, 0))
    return pl.pallas_call(
        functools.partial(attention_kernel, rows),
        grid=(pairs,),
        out_shape=(
            jax.ShapeDtypeStruct((length, pairs * LANES), BF),
            jax.ShapeDtypeStruct((length, 3 * pairs * LANES), BF),
        ),
        in_specs=[
            pl.BlockSpec((length, 3 * LANES), lambda p: (0, p)),
            pl.BlockSpec((length, LANES), lambda p: (0, p)),
            whole((length, LANES)),
            whole((length, LANES)),
            whole((length, LANES)),
            whole((length, 1)),
            whole((1, length)),
        ],
        out_specs=(
            pl.BlockSpec((length, LANES), lambda p: (0, p)),
            pl.BlockSpec((length, 3 * LANES), lambda p: (0, p)),
        ),
        scratch_shapes=[pltpu.VMEM((length, LANES), BF)] * 3
        + [pltpu.VMEM((length, LANES), F32)] * 2,
        cost_estimate=pl.CostEstimate(
            flops=14 * pairs * length * length * LANES,
            bytes_accessed=pairs * length * LANES * 24,
            transcendentals=pairs * length * length,
        ),
    )(proj, grad_att, *tables, segments[:, None], segments[None, :])


def angle_tables(seg_row):
    length = seg_row.shape[0]
    position = jnp.arange(length, dtype=jnp.int32) + jnp.where(seg_row > 0, DOC_SHIFT, 0)
    inverse = 1.0 / 10000.0 ** (jnp.arange(0, ROT, 2, dtype=F32) / ROT)
    inverse = jnp.tile(inverse, LANES // (ROT // 2))
    angles = position.astype(F32)[:, None] * inverse[None, :]
    cosine, sine = jnp.cos(angles), jnp.sin(angles)
    lane = jnp.arange(LANES)[None, :] % HEAD
    low = lane < ROT // 2
    return (
        jnp.where(lane < ROT, cosine, 1.0),
        jnp.where(low, sine, 0.0),
        jnp.where((lane < ROT) & ~low, sine, 0.0),
    )


MESH = pl.DeviceIdType.MESH


def remote(src, dst, send, recv, device):
    return pltpu.make_async_remote_copy(
        src_ref=src, dst_ref=dst, send_sem=send, recv_sem=recv, device_id=device,
        device_id_type=MESH,
    )


class Place:
    def __init__(self, S, F):
        self.S, self.F, self.Q = S, F, S // 2
        self.j, self.f = lax.axis_index("seq"), lax.axis_index("fsdp")
        self.q, self.c = self.j // 2, lax.rem(self.j, 2)
        self.partner = 2 * self.q + 1 - self.c
        self.low = 1 - self.q // (self.Q // 2)
        self.side = 2 * (2 * self.low - 1)
        self.end = self.low * self.q + (1 - self.low) * (self.Q - 1 - self.q)

    def greet(self, over_fsdp, over_seq):
        barrier = pltpu.get_barrier_semaphore()

        def signal(j, f):
            pl.semaphore_signal(barrier, inc=1, device_id=(j, f), device_id_type=MESH)

        count = 0
        if over_fsdp:
            for k in range(1, self.F):
                signal(self.j, lax.rem(self.f + k, self.F))
            count += self.F - 1
        if over_seq == "all":
            for k in range(1, self.S):
                signal(lax.rem(self.j + k, self.S), self.f)
            count += self.S - 1
        elif over_seq == "line":
            signal(self.partner, self.f)

            @pl.when(self.q > 0)
            def _():
                signal(self.j - 2, self.f)

            @pl.when(self.q < self.Q - 1)
            def _():
                signal(self.j + 2, self.f)

            count += 1 + (self.q + self.Q - 1) // self.Q + (2 * self.Q - 2 - self.q) // self.Q
        pl.semaphore_wait(barrier, count)


class ShardGather:
    @staticmethod
    def scratch(F):
        n = 6 if F == 4 else F - 1
        return [pltpu.SemaphoreType.DMA((n,)), pltpu.SemaphoreType.DMA((n,)),
                pltpu.SemaphoreType.DMA]

    def __init__(self, at, src, dst, send, recv, local):
        self.at, self.src, self.dst = at, src, dst
        f, j = at.f, at.j
        self.own = pltpu.make_async_copy(src, dst.at[f], local)
        self.first, self.later, self.arrivals = [], [], []
        if at.F == 4:
            nx = f + 1 - 2 * lax.rem(f, 2)
            ny = lax.rem(f + 2, 4)
            nd = lax.rem(nx + 2, 4)
            half = src.shape[0] // 2
            a, b = pl.ds(0, half), pl.ds(half, half)
            table = ((nx, a), (nx, b), (ny, a), (ny, b))
            for i, (to, rows) in enumerate(table):
                self.first.append(
                    remote(src.at[rows], dst.at[f, rows], send.at[i], recv.at[i], (j, to))
                )
                self.arrivals.append(
                    remote(src.at[rows], dst.at[to, rows], send.at[i], recv.at[i], (j, to))
                )
            for i, (of, rows, to) in ((4, (nx, a, ny)), (5, (ny, b, nx))):
                self.later.append(
                    remote(dst.at[of, rows], dst.at[of, rows], send.at[i], recv.at[i], (j, to))
                )
                self.arrivals.append(
                    remote(dst.at[nd, rows], dst.at[nd, rows], send.at[i], recv.at[i], (j, to))
                )
        else:
            for k in range(1, at.F):
                to, of = lax.rem(f + k, at.F), lax.rem(f + at.F - k, at.F)
                self.first.append(
                    remote(src, dst.at[f], send.at[k - 1], recv.at[k - 1], (j, to))
                )
                self.arrivals.append(
                    remote(src, dst.at[of], send.at[k - 1], recv.at[k - 1], (j, to))
                )

    def start(self):
        self.own.start()
        for copy in self.first:
            copy.start()

    def relay(self):
        if self.later:
            self.arrivals[0].wait_recv()
            self.later[0].start()
            self.arrivals[3].wait_recv()
            self.later[1].start()

    def arrived(self):
        for i, copy in enumerate(self.arrivals):
            if not (self.later and i in (0, 3)):
                copy.wait_recv()
        self.own.wait()

    def finish(self):
        for copy in self.first + self.later:
            copy.wait_send()


class TokenGather:
    @staticmethod
    def scratch(S):
        Q = S // 2
        return [pltpu.SemaphoreType.DMA((2 * Q,)), pltpu.SemaphoreType.DMA((2 * Q,)),
                pltpu.SemaphoreType.DMA((S,)), pltpu.SemaphoreType.DMA]

    def __init__(self, at, src, dst, send, share, recv, local, rows=None):
        self.at, self.src, self.dst, self.rows = at, src, dst, rows
        self.send, self.share, self.recv = send, share, recv
        self.own = pltpu.make_async_copy(src, self.place(at.j), local)

    def place(self, slot):
        return self.dst.at[slot] if self.rows is None else self.dst.at[slot, self.rows]

    def onward(self, slot, source, i, by):
        to = self.place(slot)
        return remote(
            source, to, self.send.at[i], self.recv.at[slot], (self.at.j + by, self.at.f)
        )

    def given(self, slot, source, i):
        to = self.place(slot)
        return remote(
            source, to, self.share.at[i], self.recv.at[slot], (self.at.partner, self.at.f)
        )

    def own_copies(self):
        at, j = self.at, self.at.j
        return (
            self.onward(j, self.src, 0, at.side), self.onward(j, self.src, at.Q, -at.side),
            self.given(j, self.src, 0),
        )

    def start(self):
        self.own.start()
        far, near, part = self.own_copies()
        far.start()

        @pl.when(self.at.end > 0)
        def _():
            near.start()

        part.start()

    def from_near(self, d):
        at = self.at
        slot = at.j - at.side * d
        here = self.place(slot)
        return self.onward(slot, here, d, at.side), self.given(slot, here, d)

    def from_far(self, d):
        at = self.at
        slot = at.j + at.side * d
        here = self.place(slot)
        return self.onward(slot, here, at.Q + d, -at.side), self.given(slot, here, at.Q + d)

    def near(self, d):
        if d > self.at.Q // 2 - 1:
            return

        @pl.when(self.at.end >= d)
        def _():
            onward, part = self.from_near(d)
            onward.wait_recv()
            onward.start()
            part.start()

    def far(self, d):
        @pl.when(self.at.end + d <= self.at.Q - 1)
        def _():
            onward, part = self.from_far(d)
            part.wait_recv()

            @pl.when(self.at.end > 0)
            def _():
                onward.start()

            part.start()

    def arrived(self):
        for q in range(self.at.Q):
            slot = 2 * q + 1 - self.at.c
            self.given(slot, self.place(slot), 0).wait_recv()
        self.own.wait()

    def finish(self):
        at, Q = self.at, self.at.Q
        far, near, part = self.own_copies()
        far.wait_send()

        @pl.when(at.end > 0)
        def _():
            near.wait_send()

        part.wait_send()
        for d in range(1, Q):
            if d <= Q // 2 - 1:

                @pl.when(at.end >= d)
                def _():
                    onward, part = self.from_near(d)
                    onward.wait_send()
                    part.wait_send()

            @pl.when(at.end + d <= Q - 1)
            def _():
                onward, part = self.from_far(d)

                @pl.when(at.end > 0)
                def _():
                    onward.wait_send()

                part.wait_send()


class GradReduce:
    @staticmethod
    def scratch(F, rows, n):
        return [pltpu.VMEM((F, rows, n), BF), pltpu.VMEM((F - 1, rows, n), BF),
                pltpu.SemaphoreType.DMA((F - 1,)), pltpu.SemaphoreType.DMA((F - 1,))]

    def __init__(self, at, left, right, extra, made, got, send, recv):
        self.at, self.left, self.right, self.extra = at, left, right, extra
        self.made, self.got, self.send, self.recv = made, got, send, recv
        self.n = right.shape[-1]
        self.rows = left.shape[-1] // at.F
        self.tile = next(t for t in (512, 384, 256, 128) if self.n % t == 0)

    def copy(self, k):
        at = self.at
        to = lax.rem(at.f + k, at.F)
        return remote(
            self.made.at[to], self.got.at[k - 1], self.send.at[k - 1], self.recv.at[k - 1],
            (at.j, to),
        )

    def start(self):
        at, rows = self.at, self.rows
        aligned = rows % 128 == 0
        for t in range(0, self.n, self.tile) if not aligned else ():
            cols = slice(t, t + self.tile)
            full = dot_tn(self.left[...], columns(self.right, cols)).astype(BF)
            for p in range(at.F):
                self.made[p, 0:rows, cols] = full[p * rows : (p + 1) * rows, :]
        for k in list(range(1, at.F)) + [0]:
            p = lax.rem(at.f + k, at.F)
            if aligned:
                block = columns(self.left, pl.ds(pl.multiple_of(p * rows, 128), rows))
                for t in range(0, self.n, self.tile):
                    cols = slice(t, t + self.tile)
                    made = dot_tn(block, columns(self.right, cols))
                    self.made[p, 0:rows, cols] = made.astype(BF)
            if callable(self.extra):
                self.made[p, rows:, :] = self.extra()
            elif self.extra is not None:
                self.made[p, rows : rows + self.extra.shape[1], :] = self.extra[p].astype(BF)
            if k:
                self.copy(k).start()

    def finish(self, store):
        at = self.at
        for k in range(1, at.F):
            self.copy(k).wait_recv()
        for t in range(0, self.n, self.tile):
            cols = slice(t, t + self.tile)
            total = self.made[at.f, :, cols].astype(F32)
            for k in range(1, at.F):
                total += self.got[k - 1, :, cols].astype(F32)
            store(t, self.tile, total.astype(BF))
        for k in range(1, at.F):
            self.copy(k).wait_send()


EXTRA = 16


def exchange(S, F, collective_id, grads=(), shards=(), tokens=(), split=False):
    operands, in_specs = [], []
    vmem = pl.BlockSpec(memory_space=pltpu.VMEM)
    outs, out_specs, scratch = [], [], []
    shapes = []
    for left, right, extra in grads:
        rows, n = left.shape[1] // F + (0 if extra is None else EXTRA), right.shape[1]
        operands += [left, right] + ([] if extra is None else [extra])
        scratch += GradReduce.scratch(F, rows, n)
        shapes.append((rows, n))
        if split:
            outs.append(jax.ShapeDtypeStruct((rows - EXTRA, n), BF))
            outs.append(jax.ShapeDtypeStruct((EXTRA, n), BF))
        else:
            outs.append(jax.ShapeDtypeStruct((rows, n), BF))
    out_specs += [vmem] * len(outs)
    for array in shards:
        operands.append(array)
        outs.append(jax.ShapeDtypeStruct((F,) + array.shape, BF))
        out_specs.append(pl.BlockSpec(memory_space=pl.ANY))
        scratch += ShardGather.scratch(F)
    for array in tokens:
        operands.append(array)
        outs.append(jax.ShapeDtypeStruct((S,) + array.shape, BF))
        out_specs.append(pl.BlockSpec(memory_space=pl.ANY))
        scratch += TokenGather.scratch(S)
    in_specs = [vmem] * len(operands)
    n_in, n_out = len(operands), len(outs)

    def kernel(*refs):
        ins, results, rest = list(refs[:n_in]), list(refs[n_in : n_in + n_out]), list(
            refs[n_in + n_out :]
        )
        take = lambda items, n: [items.pop(0) for _ in range(n)]
        at = Place(S, F)
        jobs, stores = [], []
        for (_, _, extra), (rows, n) in zip(grads, shapes):
            left, right = take(ins, 2)
            extra_ref = None if extra is None else take(ins, 1)[0]
            jobs.append(GradReduce(at, left, right, extra_ref, *take(rest, 4)))
            target = take(results, 1)[0]
            rider_ref = take(results, 1)[0] if split else None

            def store(t, width, value, target=target, rows=rows, rider_ref=rider_ref):
                if split:
                    target[:, t : t + width] = value[: rows - EXTRA]
                    rider_ref[:, t : t + width] = value[rows - EXTRA :]
                else:
                    target[:, t : t + width] = value

            stores.append(store)
        spreads = [
            ShardGather(at, take(ins, 1)[0], take(results, 1)[0], *take(rest, 3)) for _ in shards
        ]
        lines = [
            TokenGather(at, take(ins, 1)[0], take(results, 1)[0], *take(rest, 4)) for _ in tokens
        ]
        at.greet(bool(jobs or spreads), "line" if lines else "")
        for item in lines + spreads:
            item.start()
        for job in jobs:
            job.start()
        waiting = list(spreads)
        for d in range(1, at.Q) if lines else ():
            for item in lines:
                item.near(d)
                item.far(d)
            if waiting:
                waiting.pop(0).relay()
        for item in waiting:
            item.relay()
        for job, store in zip(jobs, stores):
            job.finish(store)
        for item in spreads + lines:
            item.arrived()
            item.finish()

    flops = sum(2 * l.shape[0] * l.shape[1] * r.shape[1] for l, r, _ in grads)
    moved = sum(o.size * 2 for o in outs)
    return pl.pallas_call(
        kernel,
        out_shape=tuple(outs),
        in_specs=in_specs,
        out_specs=tuple(out_specs),
        scratch_shapes=scratch,
        compiler_params=pltpu.CompilerParams(
            collective_id=collective_id, has_side_effects=True
        ),
        cost_estimate=pl.CostEstimate(
            flops=flops, bytes_accessed=20 * moved, transcendentals=0
        ),
    )(*operands)


LN_ROWS = 8


class Loads:
    def __init__(self, sources, buffers, sems):
        self.copies = [
            pltpu.make_async_copy(src, buf, sems.at[i])
            for i, (src, buf) in enumerate(zip(sources, buffers))
        ]
        self.buffers = buffers

    def start(self):
        for copy in self.copies:
            copy.start()

    def ready(self, *which):
        for i in which:
            self.copies[i].wait()


class LineSum:
    @staticmethod
    def scratch(S, t, d):
        Q = S // 2
        return [pltpu.VMEM((Q, t, d), BF), pltpu.VMEM((Q + 1, t, d), BF),
                pltpu.SemaphoreType.DMA((2 * Q,)), pltpu.SemaphoreType.DMA((2 * Q,)),
                pltpu.SemaphoreType.DMA((Q,)), pltpu.SemaphoreType.DMA((Q,))]

    def __init__(self, at, part, result, pair, got, s_line, r_line, s_pair, r_pair):
        self.at, self.part, self.result, self.pair, self.got = at, part, result, pair, got
        self.s_line, self.r_line, self.s_pair, self.r_pair = s_line, r_line, s_pair, r_pair

    def share(self, slot):
        at = self.at
        return remote(
            self.part.at[2 * slot + 1 - at.c], self.pair.at[slot], self.s_pair.at[slot],
            self.r_pair.at[slot], (at.partner, at.f),
        )

    def hop(self, slot, up, last):
        at = self.at
        i = slot + (1 - up) * at.Q
        into = slot + last * (at.Q - slot)
        return remote(
            self.pair.at[slot], self.got.at[into], self.s_line.at[i], self.r_line.at[i],
            (at.j + 4 * up - 2, at.f),
        )

    def last(self, slot, up):
        at = self.at
        return (1 - up) * (1 - (at.q - 1 - slot + at.Q - 1) // at.Q)

    def start(self):
        order = []
        for i in range(self.at.Q):
            for slot in (self.at.Q - 1 - i, i):
                if slot not in order:
                    order.append(slot)
        for slot in order:
            self.share(slot).start()

    def base(self, slot):
        self.share(slot).wait_recv()
        return self.part[2 * slot + self.at.c].astype(F32) + self.pair[slot].astype(F32)

    def pass_on(self, slot, up):
        at = self.at

        @pl.when((2 * up - 1) * (slot - at.q) > 0)
        def _():
            value = self.base(slot)
            self.hop(slot, up, 0).wait_recv()
            self.pair[slot] = (value + self.got[slot].astype(F32)).astype(BF)
            self.hop(slot, up, self.last(slot, up)).start()

    def ends(self, steps):
        at = self.at

        @pl.when(at.end == 0)
        def _():
            for i in steps:
                slot = at.low * (at.Q - 1 - i) + (1 - at.low) * i
                self.pair[slot] = self.base(slot).astype(BF)
                self.hop(slot, at.low, self.last(slot, at.low)).start()

    def near(self, i):
        at = self.at

        @pl.when(at.end > 0)
        def _():
            self.pass_on(at.low * (at.Q - 1 - i) + (1 - at.low) * i, at.low)

    def far(self, i):
        at = self.at
        self.pass_on((1 - at.low) * (at.Q - 1 - i) + at.low * i, 1 - at.low)

    def total(self):
        at = self.at
        self.result[...] = self.base(at.q)

        @pl.when(at.q > 0)
        def _():
            self.hop(at.q, 1, 0).wait_recv()
            self.result[...] += self.got[at.q].astype(F32)

        @pl.when(at.q < at.Q - 1)
        def _():
            self.hop(at.q, 0, 1).wait_recv()
            self.result[...] += self.got[at.Q].astype(F32)

    def finish(self):
        q = self.at.q
        for slot in range(self.at.Q):
            self.share(slot).wait_send()

            @pl.when(q < slot)
            def _():
                self.hop(slot, 1, 0).wait_send()

            @pl.when(q > slot)
            def _():
                self.hop(slot, 0, 0).wait_send()


class VectorSum:
    @staticmethod
    def scratch(S, F, w):
        return [
            pltpu.VMEM((F, LN_ROWS, w), F32),
            pltpu.VMEM((F, LN_ROWS, w), F32),
            pltpu.VMEM((S, LN_ROWS, w), F32),
            pltpu.SemaphoreType.DMA((F - 1,)),
            pltpu.SemaphoreType.DMA((F,)),
            pltpu.SemaphoreType.DMA((S - 1,)),
            pltpu.SemaphoreType.DMA((S,)),
        ]

    def __init__(self, at, made, by_shard, by_seq, s_f, r_f, s_s, r_s):
        self.at, self.made, self.by_shard, self.by_seq = at, made, by_shard, by_seq
        j, f, S, F = at.j, at.f, at.S, at.F
        self.over_f, self.over_s = [], []
        for k in range(1, F):
            to, of = lax.rem(f + k, F), lax.rem(f + F - k, F)
            self.over_f.append(
                (remote(made.at[to], by_shard.at[f], s_f.at[k - 1], r_f.at[f], (j, to)),
                 remote(made.at[to], by_shard.at[of], s_f.at[k - 1], r_f.at[of], (j, to)))
            )
        for k in range(1, S):
            to, of = lax.rem(j + k, S), lax.rem(j + S - k, S)
            self.over_s.append(
                (remote(by_seq.at[j], by_seq.at[j], s_s.at[k - 1], r_s.at[j], (to, f)),
                 remote(by_seq.at[j], by_seq.at[of], s_s.at[k - 1], r_s.at[of], (to, f)))
            )

    def start(self):
        for copy, _ in self.over_f:
            copy.start()
        self.by_shard[self.at.f] = self.made[self.at.f]

    def turn_to_seq(self):
        for _, arrival in self.over_f:
            arrival.wait_recv()
        total = self.by_shard[0]
        for p in range(1, self.at.F):
            total += self.by_shard[p]
        self.by_seq[self.at.j] = total
        for copy, _ in self.over_s:
            copy.start()

    def finish(self, result):
        for _, arrival in self.over_s:
            arrival.wait_recv()
        total = self.by_seq[0]
        for p in range(1, self.at.S):
            total += self.by_seq[p]
        result[...] = total
        for copy, _ in self.over_f + self.over_s:
            copy.wait_send()


def closing(
    S, F, collective_id, tok, normed, upstream, grad_mixed, attended, activated, grad_pre,
    w_dense, w_down, w_qkv, w_up, extra, standard, with_dense,
):
    L, D = normed.shape
    w = D // F
    chunk = 3 * LANES
    pairs = grad_mixed.shape[1] // chunk
    grads = [(D // F + EXTRA, chunk)] * pairs
    if with_dense:
        grads.append((attended.shape[1] // F, D))
    big = [normed, grad_mixed, attended, activated, w_dense, w_down, grad_pre, w_qkv, w_up]
    if with_dense:
        big.append(upstream)
    tile = 512
    m = len(grads)

    def kernel(*refs):
        refs = list(refs)
        take = lambda n: [refs.pop(0) for _ in range(n)]
        at = Place(S, F)
        sources = take(len(big))
        extra_ref, standard_ref = take(2)
        branches, normed_sum, ln_out = take(3)
        gathered = take(m)
        loads = Loads(sources, take(len(big)), take(1)[0])
        x, gm, att, act, wd, wdn, gp, wq, wu = loads.buffers[:9]
        jobs, packed, lines = [], [], []
        for i in range(pairs):
            cols = slice(i * chunk, (i + 1) * chunk)
            jobs.append(GradReduce(at, x, gm.at[:, cols], extra_ref.at[:, :, cols], *take(4)))
        if with_dense:
            jobs.append(GradReduce(at, att, loads.buffers[9], None, *take(4)))
        for i in range(m):
            packed.append(take(1)[0])
            lines.append(TokenGather(at, packed[i], gathered[i], *take(4)))
        parts = take(2)
        sums = [
            LineSum(at, part, res, *take(6)) for part, res in zip(parts, (branches, normed_sum))
        ]
        vectors = VectorSum(at, *take(7))
        loads.start()
        at.greet(True, "all")
        loads.ready(0, 1)
        for job in jobs[:pairs]:
            job.start()
        loads.ready(2)
        if with_dense:
            loads.ready(9)
            jobs[-1].start()
        loads.ready(3, 4, 5)

        @pl.loop(0, D // tile)
        def _(i):
            cols = pl.ds(pl.multiple_of(i * tile, tile), tile)
            made = dot(att[...], wd[:, cols]) + dot(act[...], wdn[:, cols])
            parts[0][:, :, cols] = made.astype(BF).reshape(S, tok, tile)

        sums[0].start()
        sums[0].ends([0])
        loads.ready(6, 7, 8)

        @pl.loop(0, D // tile)
        def _(i):
            rows = pl.ds(pl.multiple_of(i * tile, tile), tile)
            made = dot_nt(gm[...], wq[rows, :]) + dot_nt(gp[...], wu[rows, :])
            parts[1][:, :, rows] = made.astype(BF).reshape(S, tok, tile)

        sums[1].start()
        sums[1].ends([0])

        def reduced(i):
            def store(t, wide, value):
                packed[i][:, t : t + wide] = value

            jobs[i].finish(store)
            lines[i].start()

        for i in range(m):
            reduced(i)
            if i < 2:
                sums[i].near(0)
            lines[i].far(1)
        for i in range(m, 2):
            sums[i].near(0)
        for item in sums:
            item.ends(range(1, at.Q - 1))
        for i in range(max(m, 2)):
            if i < 2:
                sums[i].far(0)
            if i < m:
                lines[i].near(1)
        for step in range(1, at.Q - 1):
            for line in lines:
                line.far(step + 1)
            for item in sums:
                item.near(step)
            for item in sums:
                item.far(step)
            for line in lines:
                line.near(step + 1)
        for item in sums:
            item.total()
        grad_normed = normed_sum[...]
        both = jnp.concatenate(
            [
                jnp.sum(grad_normed * standard_ref[...], axis=0, keepdims=True),
                jnp.sum(grad_normed, axis=0, keepdims=True),
                jnp.zeros((LN_ROWS - 2, D), F32),
            ],
            axis=0,
        )
        for p in range(F):
            vectors.made[p] = both[:, p * w : (p + 1) * w]
        vectors.start()
        vectors.turn_to_seq()
        for line in lines:
            line.arrived()
            line.finish()
        vectors.finish(ln_out)
        for item in sums:
            item.finish()

    vmem = pl.BlockSpec(memory_space=pltpu.VMEM)
    anywhere = pl.BlockSpec(memory_space=pl.ANY)
    scratch = [pltpu.VMEM(a.shape, a.dtype) for a in big]
    scratch.append(pltpu.SemaphoreType.DMA((len(big),)))
    for rows, n in grads:
        scratch += GradReduce.scratch(F, rows, n)
    for rows, n in grads:
        scratch.append(pltpu.VMEM((rows, n), BF))
        scratch += TokenGather.scratch(S)
    scratch += [pltpu.VMEM((S, tok, D), BF)] * 2
    scratch += LineSum.scratch(S, tok, D) * 2
    scratch += VectorSum.scratch(S, F, w)
    full = jax.ShapeDtypeStruct((tok, D), F32)
    return pl.pallas_call(
        kernel,
        out_shape=(full, full, jax.ShapeDtypeStruct((LN_ROWS, w), F32))
        + tuple(jax.ShapeDtypeStruct((S, rows, n), BF) for rows, n in grads),
        in_specs=[anywhere] * len(big) + [vmem] * 2,
        out_specs=(vmem,) * 3 + (anywhere,) * m,
        scratch_shapes=scratch,
        compiler_params=pltpu.CompilerParams(
            collective_id=collective_id, has_side_effects=True,
            vmem_limit_bytes=67_000_000 if L > 1024 else None,
        ),
        cost_estimate=pl.CostEstimate(
            flops=6 * L * D * (grad_mixed.shape[1] + activated.shape[1]),
            bytes_accessed=80 * L * D,
            transcendentals=0,
        ),
    )(*big, extra, standard)


def attend_and_close(
    S, F, collective_id, tok, normed, upstream, feed_out, feed_gn, w_dense, w_qkv, rest_up, tables,
     seg_col, seg_row, bias, standard,
):
    L, D = S * tok, normed.shape[2]
    w = D // F
    chunk = 3 * LANES
    pairs = w_qkv.shape[1] // chunk
    rows_att = 256
    grads = [(D // F + EXTRA, chunk)] * pairs + [(pairs * LANES // F, D)]
    m = len(grads)
    big = [normed, upstream, w_qkv, w_dense, feed_out, feed_gn]
    small = [*tables, seg_col, seg_row, bias, standard, rest_up]
    tile = 512
    late = rest_up.shape[0]

    def kernel(*refs):
        refs = list(refs)
        take = lambda n: [refs.pop(0) for _ in range(n)]
        at = Place(S, F)
        sources = take(len(big))
        cos, low, high, seg_c, seg_r, bias_ref, standard_ref, up_ref = take(8)
        branches, normed_sum, ln_out, all_up = take(4)
        gathered = take(m)
        loads = Loads(sources, take(len(big)), take(1)[0])
        x, g, wq, wd, out_part, gn_part = loads.buffers
        gm, att, proj, gatt, qs, ks, vs, dk, dv = take(9)
        ones = jnp.ones((16, L), BF)
        jobs, lines = [], []
        for i in range(pairs):
            cols = slice(i * chunk, (i + 1) * chunk)
            total_row = lambda cols=cols: dot(ones, gm[:, cols]).astype(BF)
            jobs.append(GradReduce(at, x, gm.at[:, cols], total_row, *take(4)))
        jobs.append(GradReduce(at, att, g, None, *take(4)))
        for i in range(m):
            lines.append(TokenGather(at, jobs[i].made.at[at.f], gathered[i], *take(4)))
        ups = [
            TokenGather(at, up_ref.at[i], all_up.at[i], *take(4)) for i in range(late)
        ]
        parts = [out_part, gn_part]
        sums = [
            LineSum(at, part, res, *take(6)) for part, res in zip(parts, (branches, normed_sum))
        ]
        vectors = VectorSum(at, *take(7))
        loads.start()
        at.greet(True, "all")
        for up in ups:
            up.start()
        loads.ready(0, 1, 2, 3)

        @pl.loop(0, pairs)
        def _(p):
            cols = pl.ds(pl.multiple_of(p * chunk, LANES), chunk)
            lanes = pl.ds(pl.multiple_of(p * LANES, LANES), LANES)

            @pl.loop(0, L // rows_att)
            def _(i):
                slots = pl.ds(i * (rows_att // tok), rows_att // tok)
                rows = pl.ds(pl.multiple_of(i * rows_att, rows_att), rows_att)
                block = x[slots].reshape(rows_att, D)
                proj[rows, :] = dot(block, wq[:, cols]) + bias_ref[:, cols]
                block = g[slots].reshape(rows_att, D)
                gatt[rows, :] = dot_nt(block, wd[lanes, :]).astype(BF)

            def during(pair, *steps):
                @pl.when(p == pair)
                def _():
                    for step in steps:
                        step()

            def serve(i, d):
                return lambda: (ups[i].near(d), ups[i].far(d))

            during(0, serve(0, 1))
            during(1, serve(0, 2))

            def pause(i):
                if i == 3:
                    during(0, serve(1, 1))
                    during(1, serve(1, 2))
                if i == 2:
                    during(0, *(serve(k, 1) for k in range(2, late)))
                    during(1, *(serve(k, 2) for k in range(2, late)))

            attention_kernel(
                rows_att, proj, gatt, cos, low, high, seg_c, seg_r, att.at[:, lanes],
                gm.at[:, cols], qs, ks, vs, dk, dv, pause,
            )
            during(0, jobs[0].start)

        loads.ready(4)

        @pl.loop(0, D // tile)
        def _(i):
            cols = pl.ds(pl.multiple_of(i * tile, tile), tile)
            made = columns(out_part, cols).astype(F32) + dot(att[...], wd[:, cols])
            out_part[:, :, cols] = made.astype(BF).reshape(S, tok, tile)

        sums[0].start()
        sums[0].ends([0])
        jobs[1].start()
        loads.ready(5)

        @pl.loop(0, D // tile)
        def _(i):
            rows = pl.ds(pl.multiple_of(i * tile, tile), tile)
            made = columns(gn_part, rows).astype(F32) + dot_nt(gm[...], wq[rows, :])
            gn_part[:, :, rows] = made.astype(BF).reshape(S, tok, tile)

        sums[1].start()
        sums[1].ends([0])

        def reduced(i):
            def store(t, wide, value):
                jobs[i].made[at.f, :, t : t + wide] = value

            jobs[i].finish(store)
            lines[i].start()

        reduced(0)
        for job in jobs[2:]:
            job.start()
        for d in range(3, at.Q):
            for up in ups:
                up.near(d)
                up.far(d)
        lines[0].far(1)

        for item in sums:
            item.ends([1])
        for i in range(m):
            if i:
                reduced(i)
            if i < 2:
                sums[i].near(0)
            if i:
                lines[i].far(1)
        for item in sums:
            item.ends(range(2, at.Q - 1))
        for i in range(m):
            if i < 2:
                sums[i].far(0)
            lines[i].near(1)
        for step in range(1, at.Q - 1):
            for line in lines:
                line.far(step + 1)
            for item in sums:
                item.near(step)
            for item in sums:
                item.far(step)
            for line in lines:
                line.near(step + 1)
        for item in sums:
            item.total()
        grad_normed = normed_sum[...]
        both = jnp.concatenate(
            [
                jnp.sum(grad_normed * standard_ref[...], axis=0, keepdims=True),
                jnp.sum(grad_normed, axis=0, keepdims=True),
                jnp.zeros((LN_ROWS - 2, D), F32),
            ],
            axis=0,
        )
        for p in range(F):
            vectors.made[p] = both[:, p * w : (p + 1) * w]
        vectors.start()
        vectors.turn_to_seq()
        for line in ups + lines:
            line.arrived()
            line.finish()
        vectors.finish(ln_out)
        for item in sums:
            item.finish()

    vmem = pl.BlockSpec(memory_space=pltpu.VMEM)
    anywhere = pl.BlockSpec(memory_space=pl.ANY)
    scratch = [pltpu.VMEM(a.shape, a.dtype) for a in big]
    scratch.append(pltpu.SemaphoreType.DMA((len(big),)))
    scratch += [
        pltpu.VMEM((L, pairs * chunk), BF),
        pltpu.VMEM((L, pairs * LANES), BF),
        pltpu.VMEM((L, chunk), F32),
    ]
    scratch += [pltpu.VMEM((L, LANES), BF)] * 4 + [pltpu.VMEM((L, LANES), F32)] * 2
    for rows, n in grads:
        scratch += GradReduce.scratch(F, rows, n)
    scratch += TokenGather.scratch(S) * m
    scratch += TokenGather.scratch(S) * late
    scratch += LineSum.scratch(S, tok, D) * 2
    scratch += VectorSum.scratch(S, F, w)
    full = jax.ShapeDtypeStruct((tok, D), F32)
    return pl.pallas_call(
        kernel,
        out_shape=(
            full, full, jax.ShapeDtypeStruct((LN_ROWS, w), F32),
            jax.ShapeDtypeStruct((late, S) + rest_up.shape[1:], BF),
        )
        + tuple(jax.ShapeDtypeStruct((S, rows, n), BF) for rows, n in grads),
        in_specs=[anywhere] * len(big) + [vmem] * len(small),
        out_specs=(vmem,) * 3 + (anywhere,) * (1 + m),
        scratch_shapes=scratch,
        compiler_params=pltpu.CompilerParams(
            collective_id=collective_id, has_side_effects=True, vmem_limit_bytes=67_000_000
        ),
        cost_estimate=pl.CostEstimate(
            flops=10 * L * D * pairs * chunk,
            bytes_accessed=100 * L * D,
            transcendentals=pairs * L * L,
        ),
    )(*big, *small)


class CornerReduce:
    @staticmethod
    def scratch(rows, n):
        return [pltpu.VMEM((4, rows, n), BF), pltpu.VMEM((3, rows, n), BF),
                pltpu.SemaphoreType.DMA((3,)), pltpu.SemaphoreType.DMA((3,))]

    def __init__(self, at, axis, made, got, send, recv):
        f = at.f
        nx, ny = f + 1 - 2 * lax.rem(f, 2), lax.rem(f + 2, 4)
        self.at, self.made, self.got = at, made, got
        self.one, self.two = (nx, ny) if axis == 0 else (ny, nx)
        self.far = lax.rem(nx + 2, 4)
        self.copies = [
            remote(made.at[block], got.at[i], send.at[i], recv.at[i], (at.j, to))
            for i, (block, to) in enumerate(
                ((self.far, self.one), (self.one, self.one), (self.two, self.two))
            )
        ]

    def send(self):
        self.copies[0].start()
        self.copies[1].start()

    def make(self, make, send):
        for p in (self.far, self.one, self.two, self.at.f):
            make(p)
            if send and p is self.one:
                self.send()

    def middle(self):
        self.copies[0].wait_recv()
        block = self.made[self.two].astype(F32) + self.got[0].astype(F32)
        self.made[self.two] = block.astype(BF)
        self.copies[2].start()

    def total(self):
        self.copies[1].wait_recv()
        self.copies[2].wait_recv()
        total = self.made[self.at.f].astype(F32) + self.got[1].astype(F32)
        return (total + self.got[2].astype(F32)).astype(BF)

    def finish(self):
        for copy in self.copies:
            copy.wait_send()


SMALL = 48
CHUNKS = 4


def opening(
    S, collective_id, tok, small, tokens, cotangent, fc1_weight, fc2_weight, qkv_weight,
    dense_weight,
):
    F, Q, L = 4, S // 2, tok * S
    D, ff = tokens.shape[1], fc1_weight.shape[1]
    rows_d, cols_up = D // F, ff // S
    w_ff = cols_up // F
    pairs = HEADS // S // 2
    wide = 3 * pairs * LANES
    dense_rows = HEAD * HEADS // (F * S)
    half = S // 2
    n_down, n_up = D // CHUNKS, cols_up // CHUNKS
    lead = {}
    at_row = 0
    for name, n in (
        ("gain", rows_d), ("bias", rows_d), ("qkv", 3 * rows_d), ("dense", rows_d),
        ("up", ff // F), ("down", rows_d),
    ):
        lead[name] = (at_row, n // 128)
        at_row += n // 128

    def kernel(*refs):
        refs = list(refs)
        take = lambda n: [refs.pop(0) for _ in range(n)]
        (small_in, tok_in, cot_in, up_in, down_in, qkv_in, dense_in) = take(7)
        (o_normed, o_out, o_gn, o_g, o_qkv, o_dense, o_alldown, o_allup, o_piece,
         o_vec, o_small) = take(11)
        at = Place(S, F)
        j, f = at.j, at.f
        x_own, g_own, n_own, up_own, down_own, dense_own, qkv_raw, qkv_own = take(8)
        normed, g, w_up, w_down, act, gp, slope, part_out, part_gn = take(9)
        small_all, pieces = take(2)
        load_sem, save_sem, s_small, r_small = take(4)
        copies = []

        def load(src, dst):
            copy = pltpu.make_async_copy(src, dst, load_sem.at[len(copies)])
            copies.append(copy)
            copy.start()
            return copy

        for p in range(F):
            load(up_in.at[:, pl.ds(pl.multiple_of((p * S + j) * w_ff, w_ff), w_ff)],
                 up_own.at[:, p * w_ff : (p + 1) * w_ff])
        load(tok_in, x_own)
        load(cot_in, g_own)
        load(down_in.at[pl.ds(pl.multiple_of(j * w_ff, w_ff), w_ff)], down_own)
        load(dense_in.at[pl.ds(pl.multiple_of(j * dense_rows, dense_rows), dense_rows)],
             dense_own)
        for i in range(3 * pairs):
            for which in range(2):
                block = (i % 3) * F * half + (2 * (i // 3) + which) * half + j // 2
                load(qkv_in.at[:, pl.ds(pl.multiple_of(block * LANES, LANES), LANES)],
                     qkv_raw.at[2 * i + which])

        gathers = [
            ShardGather(at, src, dst, *take(3))
            for src, dst in (
                (up_own, w_up), (down_own, w_down), (qkv_own, o_qkv), (dense_own, o_dense),
            )
        ]
        line_n = TokenGather(at, n_own, normed, *take(4))
        line_g = TokenGather(at, g_own, g, *take(4))
        reduce_down = [CornerReduce(at, i % 2, *take(4)) for i in range(CHUNKS)]
        reduce_up = [CornerReduce(at, i % 2, *take(4)) for i in range(CHUNKS)]
        lines = [
            TokenGather(at, pieces.at[i], o_alldown.at[i], *take(4)) for i in range(CHUNKS)
        ]
        lines.append(TokenGather(at, reduce_up[0].made.at[f], o_allup.at[0], *take(4)))
        at.greet(True, "line")
        smalls = []
        for k in range(1, F):
            to, of = lax.rem(f + k, F), lax.rem(f + F - k, F)
            smalls.append(
                (remote(small_in, small_all.at[f], s_small.at[k - 1], r_small.at[k - 1], (j, to)),
                 remote(small_in, small_all.at[of], s_small.at[k - 1], r_small.at[k - 1], (j, to)))
            )
        for copy, _ in smalls:
            copy.start()
        small_all[f] = small_in[...]
        for p in range(F):
            copies[p].wait()
        gathers[0].start()
        copies[F + 2].wait()
        gathers[1].start()
        copies[F + 3].wait()
        copies[F + 1].wait()
        line_g.start()

        def row_of(name):
            first, n = lead[name]
            return jnp.concatenate(
                [small_all[p, first + r : first + r + 1, :] for p in range(F) for r in range(n)],
                axis=1,
            )

        copies[F].wait()
        values = x_own[...].astype(F32)
        centre = jnp.mean(values, axis=-1, keepdims=True)
        values = values - centre
        inv_std = lax.rsqrt(jnp.mean(values * values, axis=-1, keepdims=True) + EPS)
        values = values * inv_std
        for _, arrival in smalls:
            arrival.wait_recv()
        n_own[...] = (values * row_of("gain") + row_of("bias")).astype(BF)
        line_n.start()

        for d in range(1, Q - 1):
            line_g.near(d)
            line_g.far(d)
            if d == 1:
                gathers[0].relay()
            line_n.near(d)
            line_n.far(d)
            if d == 1:
                gathers[1].relay()
                gathers[3].start()
        odd = lax.rem(j, 2) == 1
        lane = lax.broadcasted_iota(jnp.int32, (rows_d, LANES), 1)
        for copy in copies[F + 4 :]:
            copy.wait()
        for i in range(3 * pairs):
            first, second = qkv_raw[2 * i].astype(F32), qkv_raw[2 * i + 1].astype(F32)
            first = jnp.where(odd, pltpu.roll(first, HEAD, 1), first)
            second = jnp.where(odd, second, pltpu.roll(second, HEAD, 1))
            qkv_own[:, i * LANES : (i + 1) * LANES] = jnp.where(
                lane < HEAD, first, second
            ).astype(BF)
        line_g.far(Q - 1)
        gathers[3].relay()
        line_n.far(Q - 1)
        line_n.arrived()
        gathers[0].arrived()
        saves = []

        def save(src, dst):
            copy = pltpu.make_async_copy(src, dst, save_sem.at[len(saves)])
            saves.append(copy)
            copy.start()

        save(normed, o_normed)
        up_first = lead["up"][0]

        @pl.loop(0, F)
        def _(p):
            cols = pl.ds(pl.multiple_of(p * w_ff, w_ff), w_ff)
            u = jnp.concatenate(
                [
                    small_all[p, pl.ds(up_first + j * (w_ff // 128) + r, 1), :]
                    for r in range(w_ff // 128)
                ],
                axis=1,
            )
            for s in range(F):
                part = normed[:, :, s * rows_d : (s + 1) * rows_d].reshape(L, rows_d)
                u = u + dot(part, w_up[s, :, cols])
            square = u * u
            root = 0.7978845608028654
            t = jnp.tanh(root * (u + 0.044715 * (square * u)))
            act[:, cols] = ((0.5 * u) * (1.0 + t)).astype(BF)
            slope[:, cols] = 0.5 * (1.0 + t) + (0.5 * u) * (1.0 - t * t) * (
                root * (1.0 + 3 * 0.044715 * square)
            )

        line_g.arrived()
        save(g, o_g)
        ones = jnp.ones((EXTRA, L), BF)

        def make_down(c):
            cols = slice(c * n_down, (c + 1) * n_down)

            def make(p):
                block = act[:, pl.ds(pl.multiple_of(p * w_ff, w_ff), w_ff)]
                right = g[:, :, cols].reshape(L, n_down)
                reduce_down[c].made[p, 0:w_ff, :] = dot_tn(block, right).astype(BF)
                if c == 0:
                    mine = g[:, :, pl.ds(pl.multiple_of(p * rows_d, rows_d), rows_d)]
                    term = dot(ones, mine.reshape(L, rows_d))
                    reduce_down[c].made[p, w_ff:, :] = term.astype(BF)

            return make

        def make_up(c):
            cols = slice(c * n_up, (c + 1) * n_up)

            def make(p):
                block = normed[:, :, pl.ds(pl.multiple_of(p * rows_d, rows_d), rows_d)]
                made = dot_tn(block.reshape(L, rows_d), gp[:, cols])
                reduce_up[c].made[p, 0:rows_d, :] = made.astype(BF)
                if c == 0:
                    term = dot(ones, gp[:, pl.ds(pl.multiple_of(p * w_ff, w_ff), w_ff)])
                    reduce_up[c].made[p, rows_d:, :] = term.astype(BF)

            return make

        for c in range(CHUNKS):
            reduce_down[c].make(make_down(c), c < 2)
        gathers[1].arrived()

        @pl.loop(0, F)
        def _(p):
            cols = pl.ds(pl.multiple_of(p * w_ff, w_ff), w_ff)
            grad_act = dot_nt(g[...].reshape(L, D), w_down[p])
            gp[:, cols] = (grad_act * slope[:, cols]).astype(BF)


        def end_down(c):
            total = reduce_down[c].total()
            pieces[c] = total[0:w_ff, :]
            if c == 0:
                o_vec[...] = total[w_ff:, :]
            lines[c].start()

        def end_up(c):
            total = reduce_up[c].total()
            if c:
                o_piece[c - 1] = total
            else:
                reduce_up[0].made[f] = total
                lines[CHUNKS].start()

        def serve(c, d):
            lines[c].near(d)
            lines[c].far(d)

        def feed_out(i):
            cols = slice(i * rows_d, (i + 1) * rows_d)
            made = dot(act[:, 0:w_ff], w_down[0, :, cols])
            for p in range(1, F):
                made = made + dot(act[:, p * w_ff : (p + 1) * w_ff], w_down[p, :, cols])
            part_out[:, :, cols] = made.astype(BF).reshape(S, tok, rows_d)

        def feed_gn(i):
            made = dot_nt(gp[...], w_up[i])
            cols = slice(i * rows_d, (i + 1) * rows_d)
            part_gn[:, :, cols] = made.astype(BF).reshape(S, tok, rows_d)

        for c in (0, 1):
            reduce_down[c].middle()
        for c in (2, 3):
            reduce_down[c].send()
        for c in (0, 1):
            reduce_up[c].make(make_up(c), False)
        for c in (0, 1):
            end_down(c)
        for c in (2, 3):
            reduce_up[c].make(make_up(c), False)
        serve(0, 1)
        for c in (2, 3):
            reduce_down[c].middle()
        for c in (0, 1):
            reduce_up[c].send()
        serve(1, 1)
        feed_out(0)
        feed_out(1)
        for c in (2, 3):
            end_down(c)
        feed_out(2)
        serve(0, 2)
        for c in (0, 1):
            reduce_up[c].middle()
        for c in (2, 3):
            reduce_up[c].send()
        gathers[2].start()
        serve(1, 2)
        feed_out(3)
        save(part_out, o_out)
        serve(2, 1)
        for c in (0, 1):
            end_up(c)
        feed_gn(0)
        serve(3, 1)
        feed_gn(1)
        for d in range(3, Q):
            serve(0, d)
            serve(1, d)
        for c in (2, 3):
            reduce_up[c].middle()
        feed_gn(2)
        serve(2, 2)
        feed_gn(3)
        save(part_gn, o_gn)
        serve(3, 2)
        serve(CHUNKS, 1)
        gathers[2].relay()
        for c in (2, 3):
            end_up(c)
        for d in range(3, Q):
            serve(2, d)
            serve(3, d)
        for d in range(2, Q):
            serve(CHUNKS, d)
        o_small[...] = small_all[...]
        for copy, _ in smalls:
            copy.wait_send()
        for gather in gathers[2:]:
            gather.arrived()
        for line in lines:
            line.arrived()
        for item in [line_n, line_g] + lines + gathers + reduce_down + reduce_up:
            item.finish()
        for copy in saves:
            copy.wait()

    vmem = pl.BlockSpec(memory_space=pltpu.VMEM)
    anywhere = pl.BlockSpec(memory_space=pl.ANY)
    out = lambda shape, dtype=BF: jax.ShapeDtypeStruct(shape, dtype)
    scratch = [
        pltpu.VMEM(shape, dtype)
        for shape, dtype in (
            ((tok, D), BF), ((tok, D), BF), ((tok, D), BF), ((rows_d, cols_up), BF),
            ((w_ff, D), BF), ((dense_rows, D), BF), ((6 * pairs, rows_d, LANES), BF),
            ((rows_d, wide), BF),
            ((S, tok, D), BF), ((S, tok, D), BF), ((F, rows_d, cols_up), BF), ((F, w_ff, D), BF),
            ((L, cols_up), BF), ((L, cols_up), BF), ((L, cols_up), F32),
            ((S, tok, D), BF), ((S, tok, D), BF),
            ((F, SMALL, 128), F32), ((CHUNKS, w_ff, n_down), BF),
        )
    ]
    scratch += [
        pltpu.SemaphoreType.DMA((F + 4 + 6 * pairs,)), pltpu.SemaphoreType.DMA((6,)),
        pltpu.SemaphoreType.DMA((F - 1,)), pltpu.SemaphoreType.DMA((F - 1,)),
    ]
    for _ in range(4):
        scratch += ShardGather.scratch(F)
    for _ in range(2):
        scratch += TokenGather.scratch(S)
    for c in range(CHUNKS):
        scratch += CornerReduce.scratch(w_ff + (0 if c else EXTRA), n_down)
    for c in range(CHUNKS):
        scratch += CornerReduce.scratch(rows_d + (0 if c else EXTRA), n_up)
    for _ in range(CHUNKS + 1):
        scratch += TokenGather.scratch(S)
    return pl.pallas_call(
        kernel,
        out_shape=(
            out((S, tok, D)), out((S, tok, D)), out((S, tok, D)), out((S, tok, D)),
            out((F, rows_d, wide)), out((F, dense_rows, D)),
            out((CHUNKS, S, w_ff, n_down)), out((1, S, rows_d + EXTRA, n_up)),
            out((CHUNKS - 1, rows_d, n_up)),
            out((EXTRA, n_down)), out((F, SMALL, 128), F32),
        ),
        in_specs=[vmem] + [anywhere] * 6,
        out_specs=(anywhere,) * 8 + (vmem,) * 3,
        scratch_shapes=scratch,
        compiler_params=pltpu.CompilerParams(
            collective_id=collective_id, has_side_effects=True, vmem_limit_bytes=67_000_000
        ),
        cost_estimate=pl.CostEstimate(
            flops=8 * L * D * cols_up, bytes_accessed=200 * L * D, transcendentals=L * cols_up
        ),
    )(small, tokens, cotangent, fc1_weight, fc2_weight, qkv_weight, dense_weight)


def half_lanes(first, second, odd):
    lane = lax.broadcasted_iota(jnp.int32, first.shape, 1)
    if odd:
        first = pltpu.roll(first, HEAD, 1)
    else:
        second = pltpu.roll(second, HEAD, 1)
    return jnp.where(lane < HEAD, first, second)


def pick_qkv(weight, j, F, S, pairs):
    rows = weight.shape[0]
    per_shard = S // 2

    def kernel(j_ref, first, second, out):
        a, b = first[...].astype(F32), second[...].astype(F32)

        @pl.when(j_ref[0] % 2 == 0)
        def _():
            out[...] = half_lanes(a, b, 0).astype(BF)

        @pl.when(j_ref[0] % 2 == 1)
        def _():
            out[...] = half_lanes(a, b, 1).astype(BF)

    def column(which):
        return lambda i, j_ref: (
            0, (i % 3) * F * per_shard + (2 * (i // 3) + which) * per_shard + j_ref[0] // 2
        )

    return pl.pallas_call(
        kernel,
        grid_spec=pltpu.PrefetchScalarGridSpec(
            num_scalar_prefetch=1,
            grid=(3 * pairs,),
            in_specs=[pl.BlockSpec((rows, LANES), column(0)), pl.BlockSpec((rows, LANES), column(1))],
            out_specs=pl.BlockSpec((rows, LANES), lambda i, j_ref: (0, i)),
        ),
        out_shape=jax.ShapeDtypeStruct((rows, 3 * pairs * LANES), BF),
    )(j[None].astype(jnp.int32), weight, weight)


def pick_up(weight, j, F, S):
    rows, ff = weight.shape
    w = ff // (F * S)
    if w % LANES:
        split = weight.reshape(rows, F, S, w)
        return lax.dynamic_index_in_dim(split, j, 2, keepdims=False).reshape(rows, F * w)

    def kernel(j_ref, src, out):
        out[...] = src[...]

    return pl.pallas_call(
        kernel,
        grid_spec=pltpu.PrefetchScalarGridSpec(
            num_scalar_prefetch=1,
            grid=(F,),
            in_specs=[pl.BlockSpec((rows, w), lambda i, j_ref: (0, i * S + j_ref[0]))],
            out_specs=pl.BlockSpec((rows, w), lambda i, j_ref: (0, i)),
        ),
        out_shape=jax.ShapeDtypeStruct((rows, F * w), BF),
    )(j[None].astype(jnp.int32), weight)


def unpack_qkv(gathered, rows, S):
    width = S * HEAD
    pairs = len(gathered)

    def kernel(*refs):
        out = refs[pairs]
        for p in range(pairs):

            @pl.when(pl.program_id(0) % pairs == p)
            def _():
                src = refs[p]
                for half in range(2):
                    for z in range(S // 2):
                        a, b = src[2 * z].astype(F32), src[2 * z + 1].astype(F32)
                        at = half * width + z * LANES
                        out[:, at : at + LANES] = half_lanes(a, b, half)

    return pl.pallas_call(
        kernel,
        grid=(3 * pairs,),
        in_specs=[pl.BlockSpec((S, rows, LANES), lambda i: (0, 0, i // pairs))] * pairs,
        out_specs=pl.BlockSpec((rows, 2 * width), lambda i: (0, i)),
        out_shape=jax.ShapeDtypeStruct((rows, HEADS * HEAD * 3), F32),
    )(*gathered)


def unpack_groups(*stacks, rows):
    S, w = stacks[0].shape[1], stacks[0].shape[3]
    groups = [stack.shape[0] for stack in stacks]
    starts = [sum(groups[:i]) for i in range(len(groups))]

    def kernel(*refs):
        i = pl.program_id(0)
        for src, start, count in zip(refs, starts, groups):

            @pl.when((i >= start) & (i < start + count))
            def _():
                for s in range(S):
                    refs[-1][:, s * w : (s + 1) * w] = src[0, s].astype(F32)

    def block(start, count):
        return pl.BlockSpec(
            (1, S, rows, w), lambda i: (jnp.clip(i - start, 0, count - 1), 0, 0, 0)
        )

    return pl.pallas_call(
        kernel,
        grid=(sum(groups),),
        in_specs=[block(start, count) for start, count in zip(starts, groups)],
        out_specs=pl.BlockSpec((rows, S * w), lambda i: (0, i)),
        out_shape=jax.ShapeDtypeStruct((rows, sum(groups) * S * w), F32),
    )(*stacks)


def unpack_cols(gathered, rows, F):
    S, _, cols = gathered.shape
    w = cols // F
    if w % LANES:
        split = gathered[:, :rows].reshape(S, rows, F, w)
        return split.transpose(1, 2, 0, 3).reshape(rows, F * S * w).astype(F32)

    def kernel(src, out):
        for s in range(S):
            out[:, s * w : (s + 1) * w] = src[s].astype(F32)

    return pl.pallas_call(
        kernel,
        grid=(F,),
        in_specs=[pl.BlockSpec((S, rows, w), lambda i: (0, 0, i))],
        out_specs=pl.BlockSpec((rows, S * w), lambda i: (0, i)),
        out_shape=jax.ShapeDtypeStruct((rows, F * S * w), F32),
    )(gathered)


def unpack_chunks(gathered):
    C, S, rows, n = gathered.shape

    def kernel(src, out):
        for c in range(C):
            out[:, c * n : (c + 1) * n] = src[c, 0].astype(F32)

    return pl.pallas_call(
        kernel,
        grid=(S,),
        in_specs=[pl.BlockSpec((C, 1, rows, n), lambda i: (0, i, 0, 0))],
        out_specs=pl.BlockSpec((rows, C * n), lambda i: (i, 0)),
        out_shape=jax.ShapeDtypeStruct((S * rows, C * n), F32),
    )(gathered)


def unpack_rows(gathered, rows):
    S, _, n = gathered.shape

    def kernel(src, out):
        out[...] = src[0].astype(F32)

    return pl.pallas_call(
        kernel,
        grid=(S,),
        in_specs=[pl.BlockSpec((1, rows, n), lambda i: (i, 0, 0))],
        out_specs=pl.BlockSpec((rows, n), lambda i: (i, 0)),
        out_shape=jax.ShapeDtypeStruct((S * rows, n), F32),
    )(gathered)


def body(
    tokens,
    ln_gain,
    ln_bias,
    qkv_weight,
    qkv_bias,
    dense_weight,
    dense_bias,
    fc1_weight,
    fc1_bias,
    fc2_weight,
    fc2_bias,
    segments,
    positions,
    cotangent,
):
    S, F = lax.axis_size("seq"), lax.axis_size("fsdp")
    j, f = lax.axis_index("seq"), lax.axis_index("fsdp")
    tok, D = tokens.shape[1], tokens.shape[2]
    length = tok * S
    rows_d = D // F
    ff = fc1_weight.shape[1]
    cols_up = ff // S
    block_up = cols_up // F
    hp = HEADS // S
    pairs = hp // 2
    per_shard = HEADS // F
    spread = per_shard % S == 0
    slots = per_shard // S if spread else 0

    qkv_width = pairs * 3 * LANES

    def heads_of(array, lead):
        shape = array.shape
        if spread:
            split = array.reshape(shape[:lead] + (F, S, slots) + shape[lead + 1 :])
            mine = lax.dynamic_index_in_dim(split, j, lead + 1, keepdims=False)
            return mine.reshape(shape[:lead] + (hp,) + shape[lead + 1 :])
        return lax.dynamic_slice_in_dim(array, j * hp, hp, lead)

    def qkv_cols(array):
        n = array.shape[0]
        mine = heads_of(array.reshape(n, 3, HEADS, HEAD), 2)
        return mine.reshape(n, 3, pairs, 2, HEAD).transpose(0, 2, 1, 3, 4).reshape(n, -1)

    def from_qkv_cols(gathered):
        n = gathered.shape[1]
        split = gathered.reshape(S, n, pairs, 3, 2, HEAD).transpose(0, 1, 3, 2, 4, 5)
        split = split.reshape(S, n, 3, hp, HEAD)
        if spread:
            moved = jnp.moveaxis(split.reshape(S, n, 3, F, slots, HEAD), 0, 3)
        else:
            moved = jnp.moveaxis(split, 0, 2)
        return moved.reshape(n, -1)

    inputs = tokens[0].astype(F32)
    centre = jnp.mean(inputs, axis=-1, keepdims=True)
    variance = jnp.mean((inputs - centre) ** 2, axis=-1, keepdims=True)
    inv_std = lax.rsqrt(variance + EPS)
    standard = (inputs - centre) * inv_std
    upstream_own = cotangent[0]
    seg_row = segments[0]
    block_dense = slots * HEAD

    def rider(values, width):
        return jnp.pad(values[:, None], ((0, 0), (0, EXTRA - 1), (0, width - values.shape[1])))

    def split_small(small):
        cuts, at = [], 0
        for piece in smalls:
            cuts.append(small[:, at : at + piece.shape[0]].reshape(-1).astype(F32))
            at += piece.shape[0]
        return cuts

    smalls = (ln_gain, ln_bias, qkv_bias, dense_bias, fc1_bias, fc2_bias)
    fused = F == 4 and spread and slots == 1 and block_up % 128 == 0
    if fused:
        rows = [piece.astype(F32).reshape(-1, 128) for piece in smalls]
        small = jnp.concatenate(rows, axis=0)
        small = jnp.pad(small, ((0, SMALL - small.shape[0]), (0, 0)))
        (normed, feed_out, feed_gn, upstream, w_qkv, w_dense, all_down, first_up, rest_up,
         out_mine, small) = opening(
            S, 1, tok, small, tokens[0], upstream_own, fc1_weight, fc2_weight, qkv_weight,
            dense_weight,
        )
        gain, shift, b_qkv, b_dense, b_up, b_down = split_small(small.reshape(F, -1))
        w_dense = [w_dense]
        out_mine = out_mine[0, :rows_d].astype(F32)
    else:
        small = jnp.concatenate(smalls)
        small = lax.all_gather(small, "fsdp", axis=0)
        gain, shift, b_qkv, b_dense, b_up, b_down = split_small(small)

        normed_own = (standard * gain + shift).astype(BF)

        up_own = pick_up(fc1_weight, j, F, S)
        down_own = lax.dynamic_slice_in_dim(fc2_weight, j * block_up, block_up, 0)
        if spread and slots == 1:
            qkv_own = pick_qkv(qkv_weight, j, F, S, pairs)
        else:
            qkv_own = qkv_cols(qkv_weight)
        w_up, w_down, normed, upstream = exchange(
            S, F, 1, shards=(up_own, down_own), tokens=(normed_own, upstream_own)
        )
        w_up, w_down = w_up.reshape(D, cols_up), w_down.reshape(cols_up, D)
        normed, upstream = normed.reshape(length, D), upstream.reshape(length, D)

        bias_up = lax.dynamic_index_in_dim(b_up.reshape(F, S, block_up), j, 1, keepdims=False)
        bias_up = bias_up.reshape(-1)

        pre_act = dot(normed, w_up) + bias_up
        activated = gelu_tanh(pre_act).astype(BF)
        out_term = jnp.sum(upstream.astype(F32), axis=0).reshape(F, rows_d)
        piece_down, out_mine = exchange(
            S, F, 2, grads=((activated, upstream, rider(out_term, D)),), split=True
        )
        out_mine = out_mine[0, :rows_d].astype(F32)

        grad_act = dot_nt(upstream, w_down)
        grad_pre = jax.vjp(gelu_tanh, pre_act)[1](grad_act)[0].astype(BF)
        up_term = jnp.sum(grad_pre.astype(F32), axis=0).reshape(F, block_up)
        shards = (qkv_own,)
        if spread:
            shards += (lax.dynamic_slice_in_dim(dense_weight, j * block_dense, block_dense, 0),)
        piece_up, w_qkv, *w_dense, all_down = exchange(
            S, F, 3, grads=((normed, grad_pre, rider(up_term, cols_up)),), shards=shards,
            tokens=(piece_down,),
        )
    bias_qkv = qkv_cols(b_qkv[None])[0]
    w_qkv = w_qkv.reshape(D, qkv_width)
    if spread:
        w_dense = w_dense[0].reshape(hp * HEAD, D)
    else:
        w_dense = lax.dynamic_slice_in_dim(
            lax.all_gather(dense_weight, "fsdp", axis=0, tiled=True), j * hp * HEAD, hp * HEAD, 0
        )
    if fused:
        branches, grad_normed, ln_mine, late_up, *gathered = attend_and_close(
            S, F, 5, tok, normed, upstream, feed_out, feed_gn, w_dense, w_qkv, rest_up,
            angle_tables(seg_row),
            seg_row[:, None], seg_row[None, :], bias_qkv[None], standard,
        )
    else:
        all_up = lax.all_gather(piece_up, "seq", axis=0)
        projected = dot(normed, w_qkv) + bias_qkv
        grad_att = dot_nt(upstream, w_dense).astype(BF)
        attended, grad_mixed = attention(projected, grad_att, angle_tables(seg_row), seg_row)
        qkv_term = jnp.sum(grad_mixed.astype(F32), axis=0)
        qkv_term = jnp.broadcast_to(qkv_term[None], (F, qkv_width))
        branches, grad_normed, ln_mine, *gathered = closing(
            S, F, 5, tok, normed, upstream, grad_mixed, attended, activated, grad_pre,
            w_dense, w_down, w_qkv, w_up, rider(qkv_term, qkv_width), standard, spread,
        )
    all_qkv = gathered[:pairs]
    result = (inputs + branches + (b_dense + b_down)).astype(BF)
    scaled = grad_normed * gain
    grad_inputs = upstream_own.astype(F32) + inv_std * (
        scaled
        - jnp.mean(scaled, axis=-1, keepdims=True)
        - standard * jnp.mean(scaled * standard, axis=-1, keepdims=True)
    )

    if fused:
        grad_down = unpack_chunks(all_down)
        grad_up = unpack_groups(first_up, late_up, rows=rows_d)
        up_mine = first_up[0, :, rows_d].astype(F32).reshape(-1)
    else:
        grad_down = unpack_rows(all_down, block_up)
        grad_up = unpack_cols(all_up, rows_d, F)
        up_mine = all_up[:, rows_d, :block_up].astype(F32).reshape(-1)
    qkv_sums = jnp.concatenate([piece[:, rows_d] for piece in all_qkv], axis=1)
    qkv_sums = from_qkv_cols(qkv_sums[:, None]).reshape(F, -1)
    qkv_mine = lax.dynamic_index_in_dim(qkv_sums, f, 0, keepdims=False).astype(F32)
    if spread and slots == 1:
        grad_qkv = unpack_qkv(all_qkv, rows_d, S)
    else:
        joined = jnp.concatenate([piece[:, :rows_d] for piece in all_qkv], axis=2)
        grad_qkv = from_qkv_cols(joined).astype(F32)
    if spread:
        grad_dense = gathered[pairs].reshape(rows_d, D).astype(F32)
    else:
        part = lax.all_gather(dot_tn(attended, upstream).astype(BF), "seq", axis=0, tiled=True)
        grad_dense = lax.psum_scatter(part, "fsdp", scatter_dimension=0, tiled=True).astype(F32)
    return (
        result[None],
        grad_inputs[None],
        ln_mine[0],
        ln_mine[1],
        grad_qkv,
        qkv_mine,
        grad_dense,
        out_mine,
        grad_up,
        up_mine,
        grad_down,
        out_mine,
    )


def solution(mesh):
    row, mat = P("fsdp"), P("fsdp", None)
    act = P("fsdp", "seq", None)
    return jax.shard_map(
        body,
        mesh=mesh,
        in_specs=(
            act, row, row, mat, row, mat, row, mat, row, mat, row, mat, P("fsdp", "seq"), act,
        ),
        out_specs=(act, act, row, row, mat, row, mat, row, mat, row, mat, row),
        check_vma=False,
    )
```

profile of v0, /device:TPU:0, one launch (start us, length us, event | category | flops | bytes accessed | tf_op | source)
XLA Modules:
  0.0 427.9 jit_solution(7727644299176164035)
XLA Ops:
  0.6 3.5 concatenate.7
  4.1 0.6 pad_convert_fusion.refs_0_
  4.8 199.1 %shard_map.220 = (bf16[8,128,2048]{2,1,0:T(8,128)(2,1)}, bf16[8,128,2048]{2,1,0:T(8,128)(2,1)}, bf16[8,128,2048]{2,1,0:T(8,128)(2,1)}, bf16[8,128,2048]{2,1,0:T(...) custom-call(f32[48,128]{1,0:T(8,128)} %pad_convert_fusion.refs_0_, ...), custom_call_target="tpu_custom_call" | custom-call | flops 17179869184 | bytes 419430400 | tf_op jit(solution)/shard_map/pallas_call | solution.py:1481
  203.9 0.1 mul.53
  204.1 3.2 fusion.5
  207.2 1.0 copy.30.refs_9_
  208.3 0.9 copy.40
  209.2 0.0 copy-start.1
  209.2 0.6 copy-done.1
  209.8 0.1 reshape_reshape_broadcast_in_dim_reshape.3
  210.0 0.7 broadcast_in_dim_squeeze_reshape.3.refs_11_
  210.6 1.2 convert_reduce_fusion
  211.8 1.3 fusion.2
  213.2 2.3 fusion.refs_12_
  215.5 165.1 %shard_map.221 = (f32[128,2048]{1,0:T(8,128)}, f32[128,2048]{1,0:T(8,128)}, f32[8,512]{1,0:T(8,128)}, bf16[3,8,512,256]{3,2,1,0:T(8,128)(2,1)}, bf16[8,528,384]{...) custom-call(bf16[8,128,2048]{2,1,0:T(8,128)(2,1)} %get-tuple-element.30.refs_0_, ...), custom_call_target="tpu_custom_call" | custom-call | flops 16106127360 | bytes 209715200 | tf_op jit(solution)/shard_map/pallas_call | solution.py:1076
  380.6 0.7 slice_bitcast_fusion
  381.3 1.7 multiply_reduce_fusion.1
  383.0 3.6 add_bitcast_fusion
  386.6 1.4 fusion.10
  388.0 11.1 %shard_map.222 = f32[512,6144]{1,0:T(8,128)} custom-call(bf16[8,528,384]{2,1,0:T(8,128)(2,1)} %get-tuple-element.41.refs_0_, bf16[8,528,384]{2,1,0:T(8,128)(2,1)} %get-tuple-element.42.refs_1_), custom_call_target="tpu_custom_call" | custom-call | tf_op jit(solution)/shard_map/pallas_call | solution.py:1582
  399.1 0.8 slice.37
  399.9 0.8 slice.36
  400.7 0.1 reshape_broadcast_in_dim.3
  400.9 0.1 reshape_reshape.11
  400.9 0.6 convert_reduce_fusion.1
  401.6 0.0 copy-done
  401.6 2.7 bitcast_convert_fusion
  404.2 0.7 slice_convert_fusion.1
  404.9 10.3 %shard_map.223 = f32[512,8192]{1,0:T(8,128)} custom-call(bf16[1,8,528,256]{3,2,1,0:T(8,128)(2,1)} %get-tuple-element.45.refs_0_, bf16[3,8,512,256]{3,2,1,0:T(8,128)(2,1)} %get-tuple-element.46.refs_1_), custom_call_target="tpu_custom_call" | custom-call | tf_op jit(solution)/shard_map/pallas_call | solution.py:1610
  415.2 1.4 slice_convert_fusion
  416.6 10.3 %shard_map.224 = f32[2048,2048]{1,0:T(8,128)} custom-call(bf16[4,8,256,512]{3,2,1,0:T(8,128)(2,1)} %get-tuple-element.47.src), custom_call_target="tpu_custom_call" | custom-call | tf_op jit(solution)/shard_map/pallas_call | solution.py:1646
  426.8 0.6 copy.44
  (24 shorter events, 0.1 us)
Async XLA Ops:
  4.8 199.2 %copy-start.2 = (s32[1,1024]{1,0:T(1,128)S(1)}, s32[1,1024]{1,0:T(1,128)}, u32[]{:S(2)}) copy-start(s32[1,1024]{1,0:T(1,128)} %refs_10_.1) | copy-start | bytes 12292
  209.2 0.6 copy-start.1
  388.0 13.6 %copy-start = (bf16[8,64,2048]{2,1,0:T(8,128)(2,1)S(1)}, bf16[8,64,2048]{2,1,0:T(8,128)(2,1)}, u32[]{:S(2)}) copy-start(bf16[8,64,2048]{2,1,0:T(8,128)(2,1)} %get-tuple-element.43) | copy-start | bytes 6291460
  404.9 21.9 %copy-start.3 = (f32[1,512]{1,0:T(1,128)}, f32[1,512]{1,0:T(1,128)S(1)}, u32[]{:S(2)}) copy-start(f32[1,512]{1,0:T(1,128)S(1)} %slice_convert_fusion.1) | copy-start | bytes 6148
where the time goes:
time: 435 us; the launch traced here: 428 us
  Pallas kernels  396 us (91%)
  other arithmetic  20.1 us (5%)
  local copies, waits for them, and re-layouts  10.7 us (2%)
    pallas_call x1, Pallas kernels, opening(): pl.pallas_call(kernel, out_shape=(out((S, tok, D)), out((S, tok, D)), out...  199 us
    pallas_call x1, Pallas kernels, attend_and_close(): pl.pallas_call(kernel, out_shape=(full, full, jax.ShapeDtypeStruct((LN_RO...  165 us
    pallas_call x1, Pallas kernels, unpack_qkv(): pl.pallas_call(kernel, grid=(3 * pairs,), in_specs=[pl.BlockSpec((S, rows...  11.1 us
    pallas_call x1, Pallas kernels, unpack_chunks(): pl.pallas_call(kernel, grid=(S,), in_specs=[pl.BlockSpec((C, 1, rows, n),...  10.3 us
    pallas_call x1, Pallas kernels, unpack_groups(): pl.pallas_call(kernel, grid=(sum(groups),), in_specs=[block(start, count)...  10.3 us

commit v1 on v0

--- a/solution.py
+++ b/solution.py
@@ -884,7 +884,7 @@
 
 def attend_and_close(
     S, F, collective_id, tok, normed, upstream, feed_out, feed_gn, w_dense, w_qkv, rest_up, tables,
-     seg_col, seg_row, bias, standard,
+    seg_col, seg_row, bias, standard, inv_std, tokens, cotangent, gain, out_bias,
 ):
     L, D = S * tok, normed.shape[2]
     w = D // F
@@ -894,7 +894,7 @@
     grads = [(D // F + EXTRA, chunk)] * pairs + [(pairs * LANES // F, D)]
     m = len(grads)
     big = [normed, upstream, w_qkv, w_dense, feed_out, feed_gn]
-    small = [*tables, seg_col, seg_row, bias, standard, rest_up]
+    small = [*tables, seg_col, seg_row, bias, standard, inv_std, tokens, cotangent, gain, out_bias, rest_up]
     tile = 512
     late = rest_up.shape[0]
 
@@ -903,9 +903,11 @@
         take = lambda n: [refs.pop(0) for _ in range(n)]
         at = Place(S, F)
         sources = take(len(big))
-        cos, low, high, seg_c, seg_r, bias_ref, standard_ref, up_ref = take(8)
-        branches, normed_sum, ln_out, all_up = take(4)
+        cos, low, high, seg_c, seg_r, bias_ref, standard_ref, inv_ref = take(8)
+        tok_ref, cot_ref, gain_ref, out_bias_ref, up_ref = take(5)
+        out_ref, grad_ref, ln_out, all_up = take(4)
         gathered = take(m)
+        branches, normed_sum = take(2)
         loads = Loads(sources, take(len(big)), take(1)[0])
         x, g, wq, wd, out_part, gn_part = loads.buffers
         gm, att, proj, gatt, qs, ks, vs, dk, dv = take(9)
@@ -921,9 +923,9 @@
         ups = [
             TokenGather(at, up_ref.at[i], all_up.at[i], *take(4)) for i in range(late)
         ]
-        parts = [out_part, gn_part]
+        parts = [gn_part, out_part]
         sums = [
-            LineSum(at, part, res, *take(6)) for part, res in zip(parts, (branches, normed_sum))
+            LineSum(at, part, res, *take(6)) for part, res in zip(parts, (normed_sum, branches))
         ]
         vectors = VectorSum(at, *take(7))
         loads.start()
@@ -972,6 +974,16 @@
             )
             during(0, jobs[0].start)
 
+        loads.ready(5)
+
+        @pl.loop(0, D // tile)
+        def _(i):
+            rows = pl.ds(pl.multiple_of(i * tile, tile), tile)
+            made = columns(gn_part, rows).astype(F32) + dot_nt(gm[...], wq[rows, :])
+            gn_part[:, :, rows] = made.astype(BF).reshape(S, tok, tile)
+
+        sums[0].start()
+        sums[0].ends([0])
         loads.ready(4)
 
         @pl.loop(0, D // tile)
@@ -980,19 +992,9 @@
             made = columns(out_part, cols).astype(F32) + dot(att[...], wd[:, cols])
             out_part[:, :, cols] = made.astype(BF).reshape(S, tok, tile)
 
-        sums[0].start()
-        sums[0].ends([0])
-        jobs[1].start()
-        loads.ready(5)
-
-        @pl.loop(0, D // tile)
-        def _(i):
-            rows = pl.ds(pl.multiple_of(i * tile, tile), tile)
-            made = columns(gn_part, rows).astype(F32) + dot_nt(gm[...], wq[rows, :])
-            gn_part[:, :, rows] = made.astype(BF).reshape(S, tok, tile)
-
         sums[1].start()
         sums[1].ends([0])
+        jobs[1].start()
 
         def reduced(i):
             def store(t, wide, value):
@@ -1034,12 +1036,11 @@
                 item.far(step)
             for line in lines:
                 line.near(step + 1)
-        for item in sums:
-            item.total()
-        grad_normed = normed_sum[...]
+        sums[0].total()
+        grad_normed, standard = normed_sum[...], standard_ref[...]
         both = jnp.concatenate(
             [
-                jnp.sum(grad_normed * standard_ref[...], axis=0, keepdims=True),
+                jnp.sum(grad_normed * standard, axis=0, keepdims=True),
                 jnp.sum(grad_normed, axis=0, keepdims=True),
                 jnp.zeros((LN_ROWS - 2, D), F32),
             ],
@@ -1048,7 +1049,16 @@
         for p in range(F):
             vectors.made[p] = both[:, p * w : (p + 1) * w]
         vectors.start()
+        scaled = grad_normed * gain_ref[...]
+        turned = (
+            scaled
+            - jnp.mean(scaled, axis=-1, keepdims=True)
+            - standard * jnp.mean(scaled * standard, axis=-1, keepdims=True)
+        )
+        grad_ref[...] = cot_ref[...].astype(F32) + inv_ref[:, 0:1] * turned
         vectors.turn_to_seq()
+        sums[1].total()
+        out_ref[...] = (tok_ref[...].astype(F32) + branches[...] + out_bias_ref[...]).astype(BF)
         for line in ups + lines:
             line.arrived()
             line.finish()
@@ -1058,7 +1068,8 @@
 
     vmem = pl.BlockSpec(memory_space=pltpu.VMEM)
     anywhere = pl.BlockSpec(memory_space=pl.ANY)
-    scratch = [pltpu.VMEM(a.shape, a.dtype) for a in big]
+    scratch = [pltpu.VMEM((tok, D), F32)] * 2
+    scratch += [pltpu.VMEM(a.shape, a.dtype) for a in big]
     scratch.append(pltpu.SemaphoreType.DMA((len(big),)))
     scratch += [
         pltpu.VMEM((L, pairs * chunk), BF),
@@ -1076,7 +1087,7 @@
     return pl.pallas_call(
         kernel,
         out_shape=(
-            full, full, jax.ShapeDtypeStruct((LN_ROWS, w), F32),
+            jax.ShapeDtypeStruct((tok, D), BF), full, jax.ShapeDtypeStruct((LN_ROWS, w), F32),
             jax.ShapeDtypeStruct((late, S) + rest_up.shape[1:], BF),
         )
         + tuple(jax.ShapeDtypeStruct((S, rows, n), BF) for rows, n in grads),
@@ -1171,7 +1182,7 @@
         take = lambda n: [refs.pop(0) for _ in range(n)]
         (small_in, tok_in, cot_in, up_in, down_in, qkv_in, dense_in) = take(7)
         (o_normed, o_out, o_gn, o_g, o_qkv, o_dense, o_alldown, o_allup, o_piece,
-         o_vec, o_small) = take(11)
+         o_vec, o_small, o_std, o_inv) = take(13)
         at = Place(S, F)
         j, f = at.j, at.f
         x_own, g_own, n_own, up_own, down_own, dense_own, qkv_raw, qkv_own = take(8)
@@ -1247,6 +1258,8 @@
         values = values - centre
         inv_std = lax.rsqrt(jnp.mean(values * values, axis=-1, keepdims=True) + EPS)
         values = values * inv_std
+        o_std[...] = values
+        o_inv[...] = jnp.broadcast_to(inv_std, (tok, 128))
         for _, arrival in smalls:
             arrival.wait_recv()
         n_own[...] = (values * row_of("gain") + row_of("bias")).astype(BF)
@@ -1486,9 +1499,10 @@
             out((CHUNKS, S, w_ff, n_down)), out((1, S, rows_d + EXTRA, n_up)),
             out((CHUNKS - 1, rows_d, n_up)),
             out((EXTRA, n_down)), out((F, SMALL, 128), F32),
+            out((tok, D), F32), out((tok, 128), F32),
         ),
         in_specs=[vmem] + [anywhere] * 6,
-        out_specs=(anywhere,) * 8 + (vmem,) * 3,
+        out_specs=(anywhere,) * 8 + (vmem,) * 5,
         scratch_shapes=scratch,
         compiler_params=pltpu.CompilerParams(
             collective_id=collective_id, has_side_effects=True, vmem_limit_bytes=67_000_000
@@ -1722,11 +1736,6 @@
             moved = jnp.moveaxis(split, 0, 2)
         return moved.reshape(n, -1)
 
-    inputs = tokens[0].astype(F32)
-    centre = jnp.mean(inputs, axis=-1, keepdims=True)
-    variance = jnp.mean((inputs - centre) ** 2, axis=-1, keepdims=True)
-    inv_std = lax.rsqrt(variance + EPS)
-    standard = (inputs - centre) * inv_std
     upstream_own = cotangent[0]
     seg_row = segments[0]
     block_dense = slots * HEAD
@@ -1748,7 +1757,7 @@
         small = jnp.concatenate(rows, axis=0)
         small = jnp.pad(small, ((0, SMALL - small.shape[0]), (0, 0)))
         (normed, feed_out, feed_gn, upstream, w_qkv, w_dense, all_down, first_up, rest_up,
-         out_mine, small) = opening(
+         out_mine, small, standard, inv_std) = opening(
             S, 1, tok, small, tokens[0], upstream_own, fc1_weight, fc2_weight, qkv_weight,
             dense_weight,
         )
@@ -1756,6 +1765,11 @@
         w_dense = [w_dense]
         out_mine = out_mine[0, :rows_d].astype(F32)
     else:
+        inputs = tokens[0].astype(F32)
+        centre = jnp.mean(inputs, axis=-1, keepdims=True)
+        variance = jnp.mean((inputs - centre) ** 2, axis=-1, keepdims=True)
+        inv_std = lax.rsqrt(variance + EPS)
+        standard = (inputs - centre) * inv_std
         small = jnp.concatenate(smalls)
         small = lax.all_gather(small, "fsdp", axis=0)
         gain, shift, b_qkv, b_dense, b_up, b_down = split_small(small)
@@ -1804,10 +1818,11 @@
             lax.all_gather(dense_weight, "fsdp", axis=0, tiled=True), j * hp * HEAD, hp * HEAD, 0
         )
     if fused:
-        branches, grad_normed, ln_mine, late_up, *gathered = attend_and_close(
+        result, grad_inputs, ln_mine, late_up, *gathered = attend_and_close(
             S, F, 5, tok, normed, upstream, feed_out, feed_gn, w_dense, w_qkv, rest_up,
             angle_tables(seg_row),
-            seg_row[:, None], seg_row[None, :], bias_qkv[None], standard,
+            seg_row[:, None], seg_row[None, :], bias_qkv[None], standard, inv_std, tokens[0],
+            upstream_own, gain[None], (b_dense + b_down)[None],
         )
     else:
         all_up = lax.all_gather(piece_up, "seq", axis=0)
@@ -1821,13 +1836,14 @@
             w_dense, w_down, w_qkv, w_up, rider(qkv_term, qkv_width), standard, spread,
         )
     all_qkv = gathered[:pairs]
-    result = (inputs + branches + (b_dense + b_down)).astype(BF)
-    scaled = grad_normed * gain
-    grad_inputs = upstream_own.astype(F32) + inv_std * (
-        scaled
-        - jnp.mean(scaled, axis=-1, keepdims=True)
-        - standard * jnp.mean(scaled * standard, axis=-1, keepdims=True)
-    )
+    if not fused:
+        result = (inputs + branches + (b_dense + b_down)).astype(BF)
+        scaled = grad_normed * gain
+        grad_inputs = upstream_own.astype(F32) + inv_std * (
+            scaled
+            - jnp.mean(scaled, axis=-1, keepdims=True)
+            - standard * jnp.mean(scaled * standard, axis=-1, keepdims=True)
+        )
 
     if fused:
         grad_down = unpack_chunks(all_down)

time: 435 us -> 430 us (0.989)
  other arithmetic: 20.1 us -> 9.19 us
where the time goes in v1:
time: 430 us; the launch traced here: 422 us
  Pallas kernels  399 us (93%)
  local copies, waits for them, and re-layouts  13.1 us (3%)
  other arithmetic  9.19 us (2%)
    pallas_call x1, Pallas kernels, opening(): pl.pallas_call(kernel, out_shape=(out((S, tok, D)), out((S, tok, D)), out...  199 us
    pallas_call x1, Pallas kernels, attend_and_close(): pl.pallas_call(kernel, out_shape=(jax.ShapeDtypeStruct((tok, D), BF), ful...  168 us
    pallas_call x1, Pallas kernels, unpack_qkv(): pl.pallas_call(kernel, grid=(3 * pairs,), in_specs=[pl.BlockSpec((S, rows...  11.1 us
    pallas_call x1, Pallas kernels, unpack_chunks(): pl.pallas_call(kernel, grid=(S,), in_specs=[pl.BlockSpec((C, 1, rows, n),...  10.4 us
    pallas_call x1, Pallas kernels, unpack_groups(): pl.pallas_call(kernel, grid=(sum(groups),), in_specs=[block(start, count)...  10.3 us

profile of v1, /device:TPU:0, one launch (start us, length us, event | category | flops | bytes accessed | tf_op | source)
XLA Modules:
  0.0 422.5 jit_solution(17692328584821701975)
XLA Ops:
  0.6 3.5 concatenate.7
  4.1 0.6 pad_convert_fusion.refs_0_
  4.8 199.5 %shard_map.220 = (bf16[8,128,2048]{2,1,0:T(8,128)(2,1)}, bf16[8,128,2048]{2,1,0:T(8,128)(2,1)}, bf16[8,128,2048]{2,1,0:T(8,128)(2,1)}, bf16[8,128,2048]{2,1,0:T(...) custom-call(f32[48,128]{1,0:T(8,128)} %pad_convert_fusion.refs_0_, ...), custom_call_target="tpu_custom_call" | custom-call | flops 17179869184 | bytes 419430400 | tf_op jit(solution)/shard_map/pallas_call | solution.py:1494
  204.2 0.1 mul.18
  204.3 0.0 copy-done.3
  204.4 3.2 fusion
  207.6 1.0 copy.30.refs_9_
  208.6 0.9 copy.40
  209.5 0.1 reshape_reshape_broadcast_in_dim_reshape.3
  209.6 0.7 broadcast_in_dim_squeeze_reshape.3.refs_11_
  210.3 0.6 copy.35
  210.9 0.6 copy.36
  211.5 167.9 %shard_map.221 = (bf16[128,2048]{1,0:T(8,128)(2,1)}, f32[128,2048]{1,0:T(8,128)}, f32[8,512]{1,0:T(8,128)}, bf16[3,8,512,256]{3,2,1,0:T(8,128)(2,1)}, bf16[8,528...) custom-call(bf16[8,128,2048]{2,1,0:T(8,128)(2,1)} %get-tuple-element.32.refs_0_, ...), custom_call_target="tpu_custom_call" | custom-call | flops 16106127360 | bytes 209715200 | tf_op jit(solution)/shard_map/pallas_call | solution.py:1087
  379.4 1.4 fusion.4
  380.8 11.1 %shard_map.222 = f32[512,6144]{1,0:T(8,128)} custom-call(bf16[8,528,384]{2,1,0:T(8,128)(2,1)} %get-tuple-element.45.refs_0_, bf16[8,528,384]{2,1,0:T(8,128)(2,1)} %get-tuple-element.46.refs_1_), custom_call_target="tpu_custom_call" | custom-call | tf_op jit(solution)/shard_map/pallas_call | solution.py:1596
  391.9 0.8 slice.37
  392.7 0.8 slice.36
  393.5 0.1 reshape_broadcast_in_dim.3
  393.6 0.1 reshape_reshape.11
  393.7 0.6 convert_reduce_fusion
  394.3 0.0 copy-done
  394.3 2.7 bitcast_convert_fusion
  397.0 0.7 slice_convert_fusion.1
  397.7 10.3 %shard_map.223 = f32[512,8192]{1,0:T(8,128)} custom-call(bf16[1,8,528,256]{3,2,1,0:T(8,128)(2,1)} %get-tuple-element.49.refs_0_, bf16[3,8,512,256]{3,2,1,0:T(8,128)(2,1)} %get-tuple-element.50.refs_1_), custom_call_target="tpu_custom_call" | custom-call | tf_op jit(solution)/shard_map/pallas_call | solution.py:1624
  408.0 1.4 slice_convert_fusion
  409.3 10.4 %shard_map.224 = f32[2048,2048]{1,0:T(8,128)} custom-call(bf16[4,8,256,512]{3,2,1,0:T(8,128)(2,1)} %get-tuple-element.51.src), custom_call_target="tpu_custom_call" | custom-call | tf_op jit(solution)/shard_map/pallas_call | solution.py:1660
  419.7 0.0 copy-done.4
  419.7 0.6 copy.46
  420.3 0.0 copy-done.2
  420.3 0.8 copy.47
  421.1 0.0 copy-done.1
  421.1 1.0 copy.48
  (19 shorter events, 0.1 us)
Async XLA Ops:
  4.8 199.6 %copy-start.3 = (s32[1,1024]{1,0:T(1,128)S(1)}, s32[1,1024]{1,0:T(1,128)}, u32[]{:S(2)}) copy-start(s32[1,1024]{1,0:T(1,128)} %refs_10_.1) | copy-start | bytes 12292
  380.8 13.6 %copy-start = (bf16[8,64,2048]{2,1,0:T(8,128)(2,1)S(1)}, bf16[8,64,2048]{2,1,0:T(8,128)(2,1)}, u32[]{:S(2)}) copy-start(bf16[8,64,2048]{2,1,0:T(8,128)(2,1)} %get-tuple-element.47) | copy-start | bytes 6291460
  397.7 22.0 %copy-start.4 = (f32[1,512]{1,0:T(1,128)}, f32[1,512]{1,0:T(1,128)S(1)}, u32[]{:S(2)}) copy-start(f32[1,512]{1,0:T(1,128)S(1)} %slice_convert_fusion.1) | copy-start | bytes 6148
  409.3 11.0 %copy-start.2 = (bf16[128,2048]{1,0:T(8,128)(2,1)S(1)}, bf16[128,2048]{1,0:T(8,128)(2,1)}, u32[]{:S(2)}) copy-start(bf16[128,2048]{1,0:T(8,128)(2,1)} %get-tuple-element.42) | copy-start | bytes 1572868
  409.3 11.8 %copy-start.1 = (f32[128,2048]{1,0:T(8,128)S(1)}, f32[128,2048]{1,0:T(8,128)}, u32[]{:S(2)}) copy-start(f32[128,2048]{1,0:T(8,128)} %get-tuple-element.43) | copy-start | bytes 3145732
